TPU v7x, 32 devices: a whole 2x2x4 slice. The times are simulated.
32 devices in a mesh: band: 8 (over z, x), grid: 4 (over y, core).
Axes of the slice: x: 2, y: 2, z: 4, core: 2. Of those that a mesh axis runs over, the one named last changes fastest.
Arguments:
- partial_density: float32 [8, 128, 128, 128], P('band', 'grid'), may hold values from 0.01 to 1
- node_index: int32 [128, 128, 128], P('grid'), may hold values from 0 to 19
- node_weight: float32 [4, 128, 128, 128], P(None, 'grid'), may hold values from 0 to 1
- node_slope: float32 [4, 128, 128, 128], P(None, 'grid'), may hold values from -6 to 6
- kernel_table: float32 [20, 20, 114], replicated, may hold values from -0.8 to 0.8, as said below
Outputs:
- potential: float32 [128, 128, 128], P('grid')
Inputs may be any that keep to these rules, and one draw needn't show every extreme that they name: node_index(r) is the node at the lower end of the interval of q0 at r; nodes node_index - 1 to node_index + 2 carry the four weights. `kernel_table`: symmetric in its first two indices.
All inputs are finite; a program needn't handle non-finite values.
Results may differ from a plain program's by a relative error of at most 0.0003.
Values sent between devices are 32-bit elements; how exact they have to be, the bound alone decides.
A program may use at most 128 MiB of HBM per device.

v0:
```python
import math
import jax
import jax.numpy as jnp
from jax import lax
from jax.sharding import PartitionSpec as P

N = 128


def frequency_of(positions, length):
    return jnp.where(positions < length // 2, positions, positions - length)


def shell_split(square_norm):
    root_value = jnp.sqrt(square_norm.astype(jnp.float32))
    shell_idx = root_value.astype(jnp.int32)
    shell_idx = shell_idx - (shell_idx * shell_idx > square_norm).astype(jnp.int32)
    shell_idx = shell_idx + ((shell_idx + 1) * (shell_idx + 1) <= square_norm).astype(jnp.int32)
    fraction = root_value - shell_idx.astype(jnp.float32)
    return (shell_idx, fraction)


def node_fields(count_nodes, intervals, weights):
    node_ids = jnp.arange(count_nodes, dtype=jnp.int32)
    summed = jnp.zeros((count_nodes,) + intervals.shape, jnp.float32)
    for offset in range(4):
        matched = node_ids[:, None, None, None] == (intervals + (offset - 1))[None]
        summed = summed + jnp.where(matched, weights[offset][None], jnp.zeros((), jnp.float32))
    return summed


def phase_table(source_idx, target_idx, modulus):
    product_mod = source_idx[:, None] * target_idx[None, :] % modulus
    angles = product_mod.astype(jnp.float32) * (2.0 * math.pi / modulus)
    return (jnp.cos(angles), jnp.sin(angles))


def contract(pattern, operand, matrix):
    return jnp.einsum(pattern, operand, matrix, precision=lax.Precision.HIGHEST)


def mirrored(values, dim):
    return jnp.roll(jnp.flip(values, dim), 1, dim)


def forward_tables(positions, plane_ids, length):
    cosine, sine = phase_table(positions, plane_ids, length)
    alternating = jnp.where(positions % 2 == 0, 1.0, -1.0).astype(jnp.float32)
    sine = jnp.where(plane_ids[None, :] == 0, -alternating[:, None], sine)
    return (cosine, sine)


def shell_weights_of(square_norm, shell_count):
    shell_ids = jnp.arange(shell_count, dtype=jnp.int32)
    shell_idx, fraction = shell_split(square_norm)
    expand = (slice(None),) + (None,) * square_norm.ndim
    lower_hit = shell_ids[expand] == shell_idx[None]
    upper_hit = shell_ids[expand] == shell_idx[None] + 1
    return jnp.where(lower_hit, 1.0 - fraction[None], 0.0) + jnp.where(
        upper_hit, fraction[None], 0.0
    )


def per_device(partial_density, node_index, node_weight, node_slope, kernel_table):
    length = N
    half = length // 2
    count_nodes = kernel_table.shape[0]
    shell_count = kernel_table.shape[2]
    planes = half // lax.axis_size("band")
    grid_part = length // lax.axis_size("grid")
    band_at = lax.axis_index("band")
    grid_at = lax.axis_index("grid")
    full_range = jnp.arange(length, dtype=jnp.int32)
    own_planes = band_at * planes + jnp.arange(planes, dtype=jnp.int32)
    own_rows = grid_at * grid_part + jnp.arange(grid_part, dtype=jnp.int32)
    first_band = band_at == 0
    lower_rows = (full_range >= 1) & (full_range < half)
    upper_rows = full_range > half
    density = lax.psum(partial_density[0], "band")
    theta_fields = density[None] * node_fields(count_nodes, node_index, node_weight)
    cosine_z, sine_z = forward_tables(full_range, own_planes, length)
    forward_real = contract("axyz,zk->axyk", theta_fields, cosine_z)
    forward_imag = -contract("axyz,zk->axyk", theta_fields, sine_z)
    columns = jnp.stack([forward_real, forward_imag])
    cosine_full, sine_full = phase_table(full_range, full_range, length)
    y_cos = contract("caxyp,yw->caxpw", columns, cosine_full)
    y_sin = contract("caxyp,yw->caxpw", columns, sine_full)
    ywave_real = y_cos[0] + y_sin[1]
    ywave_imag = y_cos[1] - y_sin[0]
    first_real = ywave_real[:, :, 0, :]
    first_imag = ywave_imag[:, :, 0, :]
    turned_real = mirrored(first_real, 2)
    turned_imag = mirrored(first_imag, 2)
    packed_real = jnp.where(
        lower_rows,
        0.5 * (first_real + turned_real),
        jnp.where(upper_rows, 0.5 * (turned_imag + first_imag), first_real),
    )
    packed_imag = jnp.where(
        lower_rows,
        0.5 * (first_imag - turned_imag),
        jnp.where(upper_rows, 0.5 * (first_real - turned_real), first_imag),
    )
    ywave_real = ywave_real.at[:, :, 0, :].set(jnp.where(first_band, packed_real, first_real))
    ywave_imag = ywave_imag.at[:, :, 0, :].set(jnp.where(first_band, packed_imag, first_imag))
    pencils = lax.all_to_all(
        jnp.stack([ywave_real, ywave_imag]), "grid", split_axis=4, concat_axis=2, tiled=True
    )
    x_cos = contract("caxpw,xv->capwv", pencils, cosine_full)
    x_sin = contract("caxpw,xv->capwv", pencils, sine_full)
    spec_real = x_cos[0] + x_sin[1]
    spec_imag = x_cos[1] - x_sin[0]
    freq_x = frequency_of(full_range, length)
    square_x = freq_x * freq_x
    freq_rows = frequency_of(own_rows, length)
    plane_square = own_planes * own_planes
    third_square = jnp.where(
        (own_planes[:, None] == 0) & (own_rows[None, :] > half), half * half, plane_square[:, None]
    )
    special_rows = ((own_rows == 0) | (own_rows == half)) & (own_planes[0] == 0)

    def mix_row(row_idx):
        row_real = lax.dynamic_index_in_dim(spec_real, row_idx, 2, keepdims=False)
        row_imag = lax.dynamic_index_in_dim(spec_imag, row_idx, 2, keepdims=False)
        freq_row = lax.dynamic_index_in_dim(freq_rows, row_idx, 0, keepdims=False)
        third_row = lax.dynamic_index_in_dim(third_square, row_idx, 1, keepdims=False)
        square_norm = third_row[:, None] + square_x[None, :] + freq_row * freq_row
        kernel = contract("abs,spx->abpx", kernel_table, shell_weights_of(square_norm, shell_count))
        out_real = contract("abpx,apx->bpx", kernel, row_real)
        out_imag = contract("abpx,apx->bpx", kernel, row_imag)
        other_norm = square_x + freq_row * freq_row + half * half
        kernel_other = contract(
            "abs,sx->abx", kernel_table, shell_weights_of(other_norm, shell_count)
        )
        flag = lax.dynamic_index_in_dim(special_rows, row_idx, 0, keepdims=False).astype(
            jnp.float32
        )
        spread = 0.5 * flag * (kernel[:, :, 0, :] - kernel_other)
        base_real = row_real[:, 0, :]
        base_imag = row_imag[:, 0, :]
        delta_real = mirrored(base_real, 1) - base_real
        delta_imag = -mirrored(base_imag, 1) - base_imag
        out_real = out_real.at[:, 0, :].add(contract("abx,ax->bx", spread, delta_real))
        out_imag = out_imag.at[:, 0, :].add(contract("abx,ax->bx", spread, delta_imag))
        return jnp.stack([out_real, out_imag])

    mixed = lax.map(mix_row, jnp.arange(grid_part, dtype=jnp.int32))
    i_cos = contract("wcbpx,xv->wcbpv", mixed, cosine_full)
    i_sin = contract("wcbpx,xv->wcbpv", mixed, sine_full)
    inverse_real = i_cos[:, 0] - i_sin[:, 1]
    inverse_imag = i_cos[:, 1] + i_sin[:, 0]
    returned = lax.all_to_all(
        jnp.stack([inverse_real, inverse_imag], axis=1),
        "grid",
        split_axis=4,
        concat_axis=0,
        tiled=True,
    )
    lower_col = lower_rows[:, None, None]
    upper_col = upper_rows[:, None, None]
    back_real = returned[:, 0, :, 0, :]
    back_imag = returned[:, 1, :, 0, :]
    flip_real = mirrored(back_real, 0)
    flip_imag = mirrored(back_imag, 0)
    joined_real = jnp.where(
        lower_col, back_real - flip_imag, jnp.where(upper_col, flip_real + back_imag, back_real)
    )
    joined_imag = jnp.where(
        lower_col, back_imag + flip_real, jnp.where(upper_col, back_real - flip_imag, back_imag)
    )
    returned = returned.at[:, 0, :, 0, :].set(jnp.where(first_band, joined_real, back_real))
    returned = returned.at[:, 1, :, 0, :].set(jnp.where(first_band, joined_imag, back_imag))
    b_cos = contract("wcbpx,wy->cbpxy", returned, cosine_full)
    b_sin = contract("wcbpx,wy->cbpxy", returned, sine_full)
    slab_real = b_cos[0] - b_sin[1]
    slab_imag = b_cos[1] + b_sin[0]
    cosine_own, sine_own = phase_table(own_planes, full_range, length)
    alternating = jnp.where(full_range % 2 == 0, 1.0, -1.0).astype(jnp.float32)
    cosine_back = jnp.where(own_planes[:, None] == 0, 1.0, 2.0 * cosine_own)
    sine_back = jnp.where(own_planes[:, None] == 0, -alternating[None, :], 2.0 * sine_own)
    scale_factor = 1.0 / float(length) ** 3
    field_parts = (
        contract("bpxy,pz->bxyz", slab_real, cosine_back)
        - contract("bpxy,pz->bxyz", slab_imag, sine_back)
    ) * scale_factor
    slopes = node_fields(count_nodes, node_index, node_slope)
    partial_potential = jnp.sum(field_parts * slopes, axis=0)
    return lax.psum(partial_potential, "band")


def solution(mesh):
    placed = (
        P("band", "grid", None, None),
        P("grid", None, None),
        P(None, "grid", None, None),
        P(None, "grid", None, None),
        P(),
    )
    return jax.shard_map(
        per_device, mesh=mesh, in_specs=placed, out_specs=P("grid", None, None), check_vma=False
    )
```

profile of v0, /device:TPU:0, one launch (start us, length us, event | category | flops | bytes accessed | tf_op | source)
XLA Modules:
  0.0 1415.7 jit_solution(10311914120012794032)
XLA Ops:
  7.3 5.1 broadcast_add_fusion.4
  17.1 98.9 %all-reduce.3.cloned.1.call-done = f32[32,128,128]{2,1,0:T(8,128)} async-done(((f32[32,128,128]{2,1,0:T(8,128)}), f32[32,128,128]{2,1,0:T(8,128)}) %all-reduce.3.cloned.1.call-update) | async-done | bytes 2097168 | tf_op jit(solution)/shard_map/psum | solution.py:79
  116.0 66.0 %fusion.70 = f32[1,20,32,128,8]{3,4,2,1,0:T(8,128)} fusion(f32[32,128,128]{2,1,0:T(8,128)} %get-tuple-element.295, s32[32,128,128]{2,1,0:T(8,128)} %get-tuple-element.309, f32[32,128,128]{2,1,0:T(8,128)} %get-tuple-element.296, s32[32,128,128]{2,1,0:T(8,128)} %get-tuple-element.310, f32[32,128,128]{2,1,0:T(8,128)} %get-tuple-element.294, ...), kind=kOutput, calls=%fused_computation.132 | convolution fusion | flops 1132476416 | bytes 21495840 | tf_op jit(solution)/shard_map/axyz,zk->axyk/dot_general | solution.py:39
  182.0 57.5 %negate_bitcast_fusion = f32[1,20,32,128,8]{3,4,2,1,0:T(8,128)} fusion(f32[32,128,128]{2,1,0:T(8,128)} %get-tuple-element.295, s32[32,128,128]{2,1,0:T(8,128)} %get-tuple-element.309, f32[32,128,128]{2,1,0:T(8,128)} %get-tuple-element.296, s32[32,128,128]{2,1,0:T(8,128)} %get-tuple-element.310, f32[32,128,128]{2,1,0:T(8,128)} %get-tuple-element.294, ...), kind=kOutput, calls=%fused_computation.123 | convolution fusion | flops 1133132800 | bytes 21496360 | tf_op jit(solution)/shard_map/axyz,zk->axyk/dot_general | solution.py:39
  239.6 7.2 fusion.61
  246.8 4.7 fusion.62
  266.0 7.4 scatter.15
  273.4 9.3 scatter.14
  287.3 17.6 %copy.61 = f32[2,20,32,8,128]{2,3,1,0,4:T(8,128)} copy(f32[2,20,32,8,128]{4,3,2,1,0:T(8,128)} %pad_maximum_fusion.1) | data formatting | bytes 10485760 | tf_op jit(solution)/shard_map/stack | solution.py:107
  304.9 23.5 %reshape.667 = f32[4,1,327680]{2,1,0:T(1,128)} reshape(f32[128,2,20,8,32]{4,3,2,1,0:T(8,128)} %bitcast.306) | data formatting | bytes 10485760
  328.4 5.1 all-to-all-start
  333.6 59.3 %all-to-all-done = f32[4,1,327680]{2,1,0:T(1,128)} async-done(((f32[4,1,327680]{2,1,0:T(1,128)}), f32[4,1,327680]{2,1,0:T(1,128)}, u32[]{:S(2)}, u32[]{:S(2)}) %all-to-all-start) | async-done | bytes 5242912 | tf_op jit(solution)/shard_map/all_to_all | solution.py:106
  393.5 17.9 %reduce.21 = f32[4,327680]{1,0:T(4,128)} reduce(f32[4,1,327680]{2,1,0:T(1,128)} %all-to-all-done, f32[]{:T(128)} %broadcast.766), dimensions={1}, to_apply=%all_to_all.26.reduce_sub_computation | reduce | bytes 10485764 | tf_op jit(solution)/shard_map/all_to_all | solution.py:106
  411.4 16.7 %reshape.668 = f32[128,2,20,8,32]{4,3,2,1,0:T(8,128)} reshape(f32[4,327680]{1,0:T(4,128)} %reduce.21) | data formatting | bytes 10485760
  428.1 25.8 %copy.142 = f32[2,20,32,8,4,32]{2,4,5,3,1,0:T(4,128)} copy(f32[2,20,32,8,4,32]{2,3,1,0,5,4:T(8,128)} %bitcast.307) | data formatting | bytes 10485760 | tf_op jit(solution)/shard_map/all_to_all | solution.py:106
  453.9 16.5 %all_to_all.29 = f32[2,20,128,8,32]{2,4,3,1,0:T(8,128)} reshape(f32[2,20,4,32,8,32]{3,2,5,4,1,0:T(4,128)} %bitcast.308) | data formatting | bytes 10485760 | tf_op jit(solution)/shard_map/all_to_all | solution.py:106
  470.4 8.7 fusion.81
  486.7 425.2 %while.20 = (s32[]{:T(128)}, f32[32,2,20,8,128]{4,3,2,1,0:T(8,128)}, s32[32]{0:T(128)S(1)}, f32[20,8,32,128]{3,2,1,0:T(8,128)}, s32[8,32]{0,1:T(8,128)S(1)}, /*i...) while((s32[]{:T(128)}, ...), condition=%wide.region_2.3_spmd.clone.clone, body=%wide.region_1.2_spmd.clone.clone.sunk | while | flops 633025536 | bytes 4581378 | solution.py:147
  911.9 7.2 fusion.79
  927.4 17.5 %copy.63 = f32[32,2,20,8,128]{0,3,2,1,4:T(8,128)} copy(f32[32,2,20,8,128]{4,3,2,1,0:T(8,128)} %pad_maximum_fusion.2) | data formatting | bytes 10485760 | tf_op jit(solution)/shard_map/stack | solution.py:153
  945.0 23.5 %reshape.669 = f32[4,1,327680]{2,1,0:T(1,128)} reshape(f32[128,2,20,8,32]{4,3,2,1,0:T(8,128)} %bitcast.309) | data formatting | bytes 10485760
  968.5 5.1 all-to-all-start.1
  973.6 6.4 slice_bitcast_fusion.6
  979.9 53.0 %all-to-all-done.1 = f32[4,1,327680]{2,1,0:T(1,128)} async-done(((f32[4,1,327680]{2,1,0:T(1,128)}), f32[4,1,327680]{2,1,0:T(1,128)}, u32[]{:S(2)}, u32[]{:S(2)}) %all-to-all-start.1) | async-done | bytes 5242912 | tf_op jit(solution)/shard_map/all_to_all | solution.py:152
  1033.0 18.3 %reduce.22 = f32[4,327680]{1,0:T(4,128)} reduce(f32[4,1,327680]{2,1,0:T(1,128)} %all-to-all-done.1, f32[]{:T(128)} %broadcast.766), dimensions={1}, to_apply=%all_to_all.30.reduce_sub_computation | reduce | bytes 10485764 | tf_op jit(solution)/shard_map/all_to_all | solution.py:152
  1051.3 16.7 %reshape.670 = f32[128,2,20,8,32]{4,3,2,1,0:T(8,128)} reshape(f32[4,327680]{1,0:T(4,128)} %reduce.22) | data formatting | bytes 10485760
  1068.0 25.5 %copy.64 = f32[4,32,2,20,8,32]{1,0,5,3,4,2:T(4,128)} copy(f32[4,32,2,20,8,32]{1,4,3,2,5,0:T(8,128)} %bitcast.310) | data formatting | bytes 10485760 | tf_op jit(solution)/shard_map/all_to_all | solution.py:152
  1093.5 16.6 %all_to_all.33 = f32[128,2,20,8,32]{0,4,2,3,1:T(8,128)} reshape(f32[4,32,2,20,8,32]{1,0,5,3,4,2:T(4,128)} %copy.64) | data formatting | bytes 10485760 | tf_op jit(solution)/shard_map/all_to_all | solution.py:152
  1112.6 5.6 copy.175
  1138.9 69.8 %fusion.68 = f32[20,32,128,128]{3,2,1,0:T(8,128)} fusion(f32[20,8,32,128]{3,2,1,0:T(8,128)S(1)} %get-tuple-element.284, s32[8]{0:T(128)S(1)} %iota_add_fusion.1, pred[8]{0:T(512)(128)(4,1)S(1)} %broadcast_compare_fusion), kind=kOutput, calls=%fused_computation.121 | convolution fusion | flops 1006649344 | bytes 44564520 | tf_op jit(solution)/shard_map/bpxy,pz->bxyz/dot_general | solution.py:39
  1208.8 95.9 %multiply_reduce_fusion.4 = f32[32,128,128]{2,1,0:T(8,128)} fusion(f32[20,32,128,128]{3,2,1,0:T(8,128)} %fusion.68, f32[32,128,128]{2,1,0:T(8,128)S(1)} %copy-done.6, f32[32,128,128]{2,1,0:T(8,128)S(1)} %copy-done.7, f32[32,128,128]{2,1,0:T(8,128)S(1)} %copy-done.5, f32[32,128,128]{2,1,0:T(8,128)S(1)} %get-tuple-element.289, ...), kind=kOutput, calls=%fused_computation.74 | convolution fusion | flops 1163411456 | bytes 63439400 | tf_op jit(solution)/shard_map/bpxy,pz->bxyz/dot_general | solution.py:39
  1304.7 100.9 %all-reduce.5.cloned.1.call-done = f32[32,128,128]{2,1,0:T(8,128)} async-done(((f32[32,128,128]{2,1,0:T(8,128)}), f32[32,128,128]{2,1,0:T(8,128)}) %all-reduce.5.cloned.1.call-update) | async-done | bytes 2097168 | tf_op jit(solution)/shard_map/psum | solution.py:188
  (1133 shorter events, 363.7 us)
Async XLA Ops:
  6.5 109.5 %all-reduce.3.cloned.1.call-start = ((), (), s32[]{:S(2)}) async-start(), calls=%async_computation.2 | async-start | bytes 4194304 | tf_op jit(solution)/shard_map/psum | solution.py:79
  7.3 6.2 copy-start.12
  7.3 174.7 %copy-start.14 = (f32[128]{0:T(128)}, f32[128]{0:T(128)S(1)}, u32[]{:S(2)}) copy-start(f32[128]{0:T(128)S(1)} %fusion.141) | copy-start | bytes 1540
  13.5 102.5 %copy-start = (s32[32,128,128]{2,1,0:T(8,128)S(1)}, s32[32,128,128]{2,1,0:T(8,128)}, u32[]{:S(2)}) copy-start(s32[32,128,128]{2,1,0:T(8,128)} %param.20) | copy-start | bytes 6291460
  239.5 7.3 copy-start.10
  239.5 7.3 copy-start.11
  328.4 64.5 %all-to-all-start = ((f32[4,1,327680]{2,1,0:T(1,128)}), f32[4,1,327680]{2,1,0:T(1,128)}, u32[]{:S(2)}, u32[]{:S(2)}) async-start(f32[4,1,327680]{2,1,0:T(1,128)} %reshape.667), calls=%async_computation | async-start | bytes 10485760 | tf_op jit(solution)/shard_map/all_to_all | solution.py:106
  470.4 8.8 copy-start.8
  483.6 3.1 copy-start.13
  911.9 7.2 copy-start.9
  968.5 64.5 %all-to-all-start.1 = ((f32[4,1,327680]{2,1,0:T(1,128)}), f32[4,1,327680]{2,1,0:T(1,128)}, u32[]{:S(2)}, u32[]{:S(2)}) async-start(f32[4,1,327680]{2,1,0:T(1,128)} %reshape.669), calls=%async_computation.1 | async-start | bytes 10485760 | tf_op jit(solution)/shard_map/all_to_all | solution.py:152
  973.5 432.0 %all-reduce.5.cloned.1.call-start = ((), (), s32[]{:S(2)}) async-start(), calls=%async_computation.3 | async-start | bytes 4194304 | tf_op jit(solution)/shard_map/psum | solution.py:188
  1138.8 69.9 %copy-start.1 = (s32[32,128,128]{2,1,0:T(8,128)S(1)}, s32[32,128,128]{2,1,0:T(8,128)}, u32[]{:S(2)}) copy-start(s32[32,128,128]{2,1,0:T(8,128)} %param.20) | copy-start | bytes 6291460
  1138.8 69.9 %copy-start.2 = (s32[32,128,128]{2,1,0:T(8,128)S(1)}, s32[32,128,128]{2,1,0:T(8,128)}, u32[]{:S(2)}) copy-start(s32[32,128,128]{2,1,0:T(8,128)} %get-tuple-element.308) | copy-start | bytes 6291460
  1138.8 69.9 %copy-start.3 = (s32[32,128,128]{2,1,0:T(8,128)S(1)}, s32[32,128,128]{2,1,0:T(8,128)}, u32[]{:S(2)}) copy-start(s32[32,128,128]{2,1,0:T(8,128)} %get-tuple-element.309) | copy-start | bytes 6291460
  1138.8 69.9 %copy-start.4 = (s32[32,128,128]{2,1,0:T(8,128)S(1)}, s32[32,128,128]{2,1,0:T(8,128)}, u32[]{:S(2)}) copy-start(s32[32,128,128]{2,1,0:T(8,128)} %get-tuple-element.310) | copy-start | bytes 6291460
  1138.8 69.9 %copy-start.5 = (f32[32,128,128]{2,1,0:T(8,128)S(1)}, f32[32,128,128]{2,1,0:T(8,128)}, u32[]{:S(2)}) copy-start(f32[32,128,128]{2,1,0:T(8,128)} %get-tuple-element.290) | copy-start | bytes 6291460
  1138.8 69.9 %copy-start.6 = (f32[32,128,128]{2,1,0:T(8,128)S(1)}, f32[32,128,128]{2,1,0:T(8,128)}, u32[]{:S(2)}) copy-start(f32[32,128,128]{2,1,0:T(8,128)} %get-tuple-element.291) | copy-start | bytes 6291460
  1138.8 69.9 %copy-start.7 = (f32[32,128,128]{2,1,0:T(8,128)S(1)}, f32[32,128,128]{2,1,0:T(8,128)}, u32[]{:S(2)}) copy-start(f32[32,128,128]{2,1,0:T(8,128)} %get-tuple-element.292) | copy-start | bytes 6291460
  1138.8 69.9 %copy-start.15 = (f32[128]{0:T(128)S(1)}, f32[128]{0:T(128)}, u32[]{:S(2)}) copy-start(f32[128]{0:T(128)} %copy-done.14) | copy-start | bytes 1540
Sparse Core Ops, SparseCore 0:
  11.0 105.0 all-reduce.2
  1304.8 100.6 all-reduce.4
where the time goes:
time: 1430 us; the launch traced here: 1420 us
  matrix products  482 us (34%)
  local copies, waits for them, and re-layouts  368 us (26%)
  waiting for transfers between devices  313 us (22%)
  loops' own time  128 us (9%)
  other arithmetic  99.7 us (7%)
    dot_general x76, matrix products, contract(): return jnp.einsum(pattern, operand, matrix, precision=lax.Precision.HIGHEST)  482 us
    another operation x1, loops' own time, per_device(): mixed = lax.map(mix_row, jnp.arange(grid_part, dtype=jnp.int32))  128 us
    psum x1, waiting for transfers between devices, per_device(): return lax.psum(partial_potential, 'band')  101 us
    psum x1, waiting for transfers between devices, per_device(): density = lax.psum(partial_density[0], 'band')  98.9 us
    unnamed x39, local copies, waits for them, and re-layouts  92 us
    all_to_all x1, waiting for transfers between devices, per_device(): lax.all_to_all(jnp.stack([ywave_real, ywave_imag]), 'grid', split_axis=4,...  59.3 us
    all_to_all x1, waiting for transfers between devices, per_device(): lax.all_to_all(jnp.stack([inverse_real, inverse_imag], axis=1), 'grid', s...  53 us
    all_to_all x3, local copies, waits for them, and re-layouts, per_device(): lax.all_to_all(jnp.stack([ywave_real, ywave_imag]), 'grid', split_axis=4,...  42.8 us
  transfers between devices with their start and end apart: 4, of which 4 were waited for; matrix products, arithmetic and copies ran while one was open for 1% of the time, Pallas kernels for 0%

commit v1 on v0

--- a/solution.py
+++ b/solution.py
@@ -76,7 +76,7 @@
     first_band = band_at == 0
     lower_rows = (full_range >= 1) & (full_range < half)
     upper_rows = full_range > half
-    density = lax.psum(partial_density[0], "band")
+    density = jnp.sum(lax.all_gather(partial_density[0], "band"), axis=0)
     theta_fields = density[None] * node_fields(count_nodes, node_index, node_weight)
     cosine_z, sine_z = forward_tables(full_range, own_planes, length)
     forward_real = contract("axyz,zk->axyk", theta_fields, cosine_z)

time: 1430 us -> 1550 us (1.084)
  waiting for transfers between devices: 313 us -> 435 us
    all_gather x0 -> x1, waiting for transfers between devices: none -> 222 us  [per_device(): density = jnp.sum(lax.all_gather(partial_density[0], 'band'), axis=0)]
    psum x1 -> x0, waiting for transfers between devices: 98.9 us -> none  [per_device(): density = lax.psum(partial_density[0], 'band')]
where the time goes in v1:
time: 1550 us; the launch traced here: 1540 us
  matrix products  474 us (31%)
  waiting for transfers between devices  435 us (28%)
  local copies, waits for them, and re-layouts  368 us (24%)
  loops' own time  128 us (8%)
  other arithmetic  109 us (7%)
    dot_general x76, matrix products, contract(): return jnp.einsum(pattern, operand, matrix, precision=lax.Precision.HIGHEST)  474 us
    all_gather x1, waiting for transfers between devices, per_device(): density = jnp.sum(lax.all_gather(partial_density[0], 'band'), axis=0)  222 us
    another operation x1, loops' own time, per_device(): mixed = lax.map(mix_row, jnp.arange(grid_part, dtype=jnp.int32))  128 us
    psum x1, waiting for transfers between devices, per_device(): return lax.psum(partial_potential, 'band')  99.8 us
    unnamed x39, local copies, waits for them, and re-layouts  92 us
    all_to_all x1, waiting for transfers between devices, per_device(): lax.all_to_all(jnp.stack([ywave_real, ywave_imag]), 'grid', split_axis=4,...  59.3 us
    all_to_all x1, waiting for transfers between devices, per_device(): lax.all_to_all(jnp.stack([inverse_real, inverse_imag], axis=1), 'grid', s...  53 us
    all_to_all x3, local copies, waits for them, and re-layouts, per_device(): lax.all_to_all(jnp.stack([ywave_real, ywave_imag]), 'grid', split_axis=4,...  42.8 us
  transfers between devices with their start and end apart: 4, of which 4 were waited for; matrix products, arithmetic and copies ran while one was open for 1% of the time, Pallas kernels for 0%

profile of v1, /device:TPU:0, one launch (start us, length us, event | category | flops | bytes accessed | tf_op | source)
XLA Modules:
  0.0 1539.0 jit_solution(18354637306341918486)
XLA Ops:
  7.3 5.1 broadcast_add_fusion.4
  17.0 222.5 %all-gather.2.cloned.1.call-done = f32[8,32,128,128]{3,2,1,0:T(8,128)} async-done(((f32[1,32,128,128]{3,2,1,0:T(8,128)}), f32[8,32,128,128]{3,2,1,0:T(8,128)}) %all-gather.2.cloned.1.call-update) | async-done | bytes 16777232 | tf_op jit(solution)/shard_map/all_gather | solution.py:79
  239.5 9.1 reduce_sum.18
  248.6 57.9 %fusion.70 = f32[1,20,32,128,8]{3,4,2,1,0:T(8,128)} fusion(f32[32,128,128]{2,1,0:T(8,128)} %get-tuple-element.295, s32[32,128,128]{2,1,0:T(8,128)} %get-tuple-element.309, f32[32,128,128]{2,1,0:T(8,128)} %get-tuple-element.296, s32[32,128,128]{2,1,0:T(8,128)} %get-tuple-element.310, f32[32,128,128]{2,1,0:T(8,128)} %get-tuple-element.294, ...), kind=kOutput, calls=%fused_computation.132 | convolution fusion | flops 1132476416 | bytes 21495840 | tf_op jit(solution)/shard_map/axyz,zk->axyk/dot_general | solution.py:39
  306.5 57.5 %negate_bitcast_fusion = f32[1,20,32,128,8]{3,4,2,1,0:T(8,128)} fusion(f32[32,128,128]{2,1,0:T(8,128)} %get-tuple-element.295, s32[32,128,128]{2,1,0:T(8,128)} %get-tuple-element.309, f32[32,128,128]{2,1,0:T(8,128)} %get-tuple-element.296, s32[32,128,128]{2,1,0:T(8,128)} %get-tuple-element.310, f32[32,128,128]{2,1,0:T(8,128)} %get-tuple-element.294, ...), kind=kOutput, calls=%fused_computation.123 | convolution fusion | flops 1133132800 | bytes 21496360 | tf_op jit(solution)/shard_map/axyz,zk->axyk/dot_general | solution.py:39
  364.0 7.2 fusion.61
  390.4 7.4 scatter.15
  397.9 9.3 scatter.14
  411.8 17.6 %copy.61 = f32[2,20,32,8,128]{2,3,1,0,4:T(8,128)} copy(f32[2,20,32,8,128]{4,3,2,1,0:T(8,128)} %pad_maximum_fusion.1) | data formatting | bytes 10485760 | tf_op jit(solution)/shard_map/stack | solution.py:107
  429.4 23.5 %reshape.667 = f32[4,1,327680]{2,1,0:T(1,128)} reshape(f32[128,2,20,8,32]{4,3,2,1,0:T(8,128)} %bitcast.305) | data formatting | bytes 10485760
  452.9 5.1 all-to-all-start
  458.1 59.3 %all-to-all-done = f32[4,1,327680]{2,1,0:T(1,128)} async-done(((f32[4,1,327680]{2,1,0:T(1,128)}), f32[4,1,327680]{2,1,0:T(1,128)}, u32[]{:S(2)}, u32[]{:S(2)}) %all-to-all-start) | async-done | bytes 5242912 | tf_op jit(solution)/shard_map/all_to_all | solution.py:106
  518.0 17.9 %reduce.21 = f32[4,327680]{1,0:T(4,128)} reduce(f32[4,1,327680]{2,1,0:T(1,128)} %all-to-all-done, f32[]{:T(128)} %broadcast.766), dimensions={1}, to_apply=%all_to_all.26.reduce_sub_computation | reduce | bytes 10485764 | tf_op jit(solution)/shard_map/all_to_all | solution.py:106
  535.9 16.7 %reshape.668 = f32[128,2,20,8,32]{4,3,2,1,0:T(8,128)} reshape(f32[4,327680]{1,0:T(4,128)} %reduce.21) | data formatting | bytes 10485760
  552.6 25.8 %copy.142 = f32[2,20,32,8,4,32]{2,4,5,3,1,0:T(4,128)} copy(f32[2,20,32,8,4,32]{2,3,1,0,5,4:T(8,128)} %bitcast.306) | data formatting | bytes 10485760 | tf_op jit(solution)/shard_map/all_to_all | solution.py:106
  578.4 16.5 %all_to_all.29 = f32[2,20,128,8,32]{2,4,3,1,0:T(8,128)} reshape(f32[2,20,4,32,8,32]{3,2,5,4,1,0:T(4,128)} %bitcast.307) | data formatting | bytes 10485760 | tf_op jit(solution)/shard_map/all_to_all | solution.py:106
  594.9 8.7 fusion.81
  611.2 425.2 %while.20 = (s32[]{:T(128)}, f32[32,2,20,8,128]{4,3,2,1,0:T(8,128)}, s32[32]{0:T(128)S(1)}, f32[20,8,32,128]{3,2,1,0:T(8,128)}, s32[8,32]{0,1:T(8,128)S(1)}, /*i...) while((s32[]{:T(128)}, ...), condition=%wide.region_2.3_spmd.clone.clone, body=%wide.region_1.2_spmd.clone.clone.sunk | while | flops 633025536 | bytes 4581378 | solution.py:147
  1036.4 7.2 fusion.79
  1051.9 17.5 %copy.63 = f32[32,2,20,8,128]{0,3,2,1,4:T(8,128)} copy(f32[32,2,20,8,128]{4,3,2,1,0:T(8,128)} %pad_maximum_fusion.2) | data formatting | bytes 10485760 | tf_op jit(solution)/shard_map/stack | solution.py:153
  1069.4 23.5 %reshape.669 = f32[4,1,327680]{2,1,0:T(1,128)} reshape(f32[128,2,20,8,32]{4,3,2,1,0:T(8,128)} %bitcast.308) | data formatting | bytes 10485760
  1092.9 5.1 all-to-all-start.1
  1098.0 6.4 slice_bitcast_fusion.6
  1104.4 53.0 %all-to-all-done.1 = f32[4,1,327680]{2,1,0:T(1,128)} async-done(((f32[4,1,327680]{2,1,0:T(1,128)}), f32[4,1,327680]{2,1,0:T(1,128)}, u32[]{:S(2)}, u32[]{:S(2)}) %all-to-all-start.1) | async-done | bytes 5242912 | tf_op jit(solution)/shard_map/all_to_all | solution.py:152
  1157.4 18.3 %reduce.22 = f32[4,327680]{1,0:T(4,128)} reduce(f32[4,1,327680]{2,1,0:T(1,128)} %all-to-all-done.1, f32[]{:T(128)} %broadcast.766), dimensions={1}, to_apply=%all_to_all.30.reduce_sub_computation | reduce | bytes 10485764 | tf_op jit(solution)/shard_map/all_to_all | solution.py:152
  1175.7 16.7 %reshape.670 = f32[128,2,20,8,32]{4,3,2,1,0:T(8,128)} reshape(f32[4,327680]{1,0:T(4,128)} %reduce.22) | data formatting | bytes 10485760
  1192.4 25.5 %copy.64 = f32[4,32,2,20,8,32]{1,0,5,3,4,2:T(4,128)} copy(f32[4,32,2,20,8,32]{1,4,3,2,5,0:T(8,128)} %bitcast.309) | data formatting | bytes 10485760 | tf_op jit(solution)/shard_map/all_to_all | solution.py:152
  1218.0 16.6 %all_to_all.33 = f32[128,2,20,8,32]{0,4,2,3,1:T(8,128)} reshape(f32[4,32,2,20,8,32]{1,0,5,3,4,2:T(4,128)} %copy.64) | data formatting | bytes 10485760 | tf_op jit(solution)/shard_map/all_to_all | solution.py:152
  1237.0 5.6 copy.174
  1263.3 69.8 %fusion.68 = f32[20,32,128,128]{3,2,1,0:T(8,128)} fusion(f32[20,8,32,128]{3,2,1,0:T(8,128)S(1)} %get-tuple-element.284, s32[8]{0:T(128)S(1)} %iota_add_fusion.1, pred[8]{0:T(512)(128)(4,1)S(1)} %broadcast_compare_fusion), kind=kOutput, calls=%fused_computation.121 | convolution fusion | flops 1006649344 | bytes 44564520 | tf_op jit(solution)/shard_map/bpxy,pz->bxyz/dot_general | solution.py:39
  1333.2 95.9 %multiply_reduce_fusion.4 = f32[32,128,128]{2,1,0:T(8,128)} fusion(f32[20,32,128,128]{3,2,1,0:T(8,128)} %fusion.68, f32[32,128,128]{2,1,0:T(8,128)S(1)} %copy-done.6, f32[32,128,128]{2,1,0:T(8,128)S(1)} %copy-done.7, f32[32,128,128]{2,1,0:T(8,128)S(1)} %copy-done.5, f32[32,128,128]{2,1,0:T(8,128)S(1)} %get-tuple-element.289, ...), kind=kOutput, calls=%fused_computation.74 | convolution fusion | flops 1163411456 | bytes 63439400 | tf_op jit(solution)/shard_map/bpxy,pz->bxyz/dot_general | solution.py:39
  1429.1 99.8 %all-reduce.2.cloned.1.call-done = f32[32,128,128]{2,1,0:T(8,128)} async-done(((f32[32,128,128]{2,1,0:T(8,128)}), f32[32,128,128]{2,1,0:T(8,128)}) %all-reduce.2.cloned.1.call-update) | async-done | bytes 2097168 | tf_op jit(solution)/shard_map/psum | solution.py:188
  (1134 shorter events, 368.3 us)
Async XLA Ops:
  6.5 233.0 %all-gather.2.cloned.1.call-start = ((), (), s32[]{:S(2)}) async-start(), calls=%async_computation.2 | async-start | bytes 18874368 | tf_op jit(solution)/shard_map/all_gather | solution.py:79
  7.3 6.2 copy-start.12
  7.3 299.2 %copy-start.14 = (f32[128]{0:T(128)}, f32[128]{0:T(128)S(1)}, u32[]{:S(2)}) copy-start(f32[128]{0:T(128)S(1)} %fusion.141) | copy-start | bytes 1540
  17.0 231.6 %copy-start = (s32[32,128,128]{2,1,0:T(8,128)S(1)}, s32[32,128,128]{2,1,0:T(8,128)}, u32[]{:S(2)}) copy-start(s32[32,128,128]{2,1,0:T(8,128)} %param.20) | copy-start | bytes 6291460
  364.0 7.3 copy-start.10
  364.0 7.3 copy-start.11
  452.9 64.5 %all-to-all-start = ((f32[4,1,327680]{2,1,0:T(1,128)}), f32[4,1,327680]{2,1,0:T(1,128)}, u32[]{:S(2)}, u32[]{:S(2)}) async-start(f32[4,1,327680]{2,1,0:T(1,128)} %reshape.667), calls=%async_computation | async-start | bytes 10485760 | tf_op jit(solution)/shard_map/all_to_all | solution.py:106
  594.9 8.7 copy-start.8
  608.1 3.1 copy-start.13
  1036.4 7.2 copy-start.9
  1092.9 64.5 %all-to-all-start.1 = ((f32[4,1,327680]{2,1,0:T(1,128)}), f32[4,1,327680]{2,1,0:T(1,128)}, u32[]{:S(2)}, u32[]{:S(2)}) async-start(f32[4,1,327680]{2,1,0:T(1,128)} %reshape.669), calls=%async_computation.1 | async-start | bytes 10485760 | tf_op jit(solution)/shard_map/all_to_all | solution.py:152
  1098.0 430.9 %all-reduce.2.cloned.1.call-start = ((), (), s32[]{:S(2)}) async-start(), calls=%async_computation.3 | async-start | bytes 4194304 | tf_op jit(solution)/shard_map/psum | solution.py:188
  1263.2 69.9 %copy-start.1 = (s32[32,128,128]{2,1,0:T(8,128)S(1)}, s32[32,128,128]{2,1,0:T(8,128)}, u32[]{:S(2)}) copy-start(s32[32,128,128]{2,1,0:T(8,128)} %param.20) | copy-start | bytes 6291460
  1263.2 69.9 %copy-start.2 = (s32[32,128,128]{2,1,0:T(8,128)S(1)}, s32[32,128,128]{2,1,0:T(8,128)}, u32[]{:S(2)}) copy-start(s32[32,128,128]{2,1,0:T(8,128)} %get-tuple-element.308) | copy-start | bytes 6291460
  1263.2 69.9 %copy-start.3 = (s32[32,128,128]{2,1,0:T(8,128)S(1)}, s32[32,128,128]{2,1,0:T(8,128)}, u32[]{:S(2)}) copy-start(s32[32,128,128]{2,1,0:T(8,128)} %get-tuple-element.309) | copy-start | bytes 6291460
  1263.2 69.9 %copy-start.4 = (s32[32,128,128]{2,1,0:T(8,128)S(1)}, s32[32,128,128]{2,1,0:T(8,128)}, u32[]{:S(2)}) copy-start(s32[32,128,128]{2,1,0:T(8,128)} %get-tuple-element.310) | copy-start | bytes 6291460
  1263.3 69.9 %copy-start.5 = (f32[32,128,128]{2,1,0:T(8,128)S(1)}, f32[32,128,128]{2,1,0:T(8,128)}, u32[]{:S(2)}) copy-start(f32[32,128,128]{2,1,0:T(8,128)} %get-tuple-element.290) | copy-start | bytes 6291460
  1263.3 69.9 %copy-start.6 = (f32[32,128,128]{2,1,0:T(8,128)S(1)}, f32[32,128,128]{2,1,0:T(8,128)}, u32[]{:S(2)}) copy-start(f32[32,128,128]{2,1,0:T(8,128)} %get-tuple-element.291) | copy-start | bytes 6291460
  1263.3 69.9 %copy-start.7 = (f32[32,128,128]{2,1,0:T(8,128)S(1)}, f32[32,128,128]{2,1,0:T(8,128)}, u32[]{:S(2)}) copy-start(f32[32,128,128]{2,1,0:T(8,128)} %get-tuple-element.292) | copy-start | bytes 6291460
  1263.3 69.9 %copy-start.15 = (f32[128]{0:T(128)S(1)}, f32[128]{0:T(128)}, u32[]{:S(2)}) copy-start(f32[128]{0:T(128)} %copy-done.14) | copy-start | bytes 1540
Sparse Core Ops, SparseCore 0:
  9.5 229.9 all-gather.1
  1429.2 99.5 all-reduce.1
